TPU v7x, 32 devices: a whole 2x2x4 slice. The times are simulated.
32 devices in a mesh: gx: 4 (over y, x), gy: 4 (over z), gz: 2 (over core).
Axes of the slice: x: 2, y: 2, z: 4, core: 2. Of those that a mesh axis runs over, the one named last changes fastest.
Arguments:
- queries: bfloat16 [16384, 1024], P(('gx', 'gy', 'gz')), may hold values from -6 to 6
- keys: bfloat16 [16384, 1024], P(('gx', 'gy', 'gz')), may hold values from -6 to 6
- values: bfloat16 [16384, 1024], P(('gx', 'gy', 'gz')), may hold values from -6 to 6
- out_grad: bfloat16 [16384, 1024], P(('gx', 'gy', 'gz')), may hold values from -0.046875 to 0.046875
- log_decay: float32 [4, 16384], P(None, ('gx', 'gy', 'gz')), may hold values from -0.8 to 0, as said below
- saved_states: bfloat16 [32, 4, 256, 256], P(('gx', 'gy', 'gz')), may hold values from -67.5 to 67.5
Outputs:
- query_grad: bfloat16 [16384, 1024], P(('gx', 'gy', 'gz'))
- key_grad: bfloat16 [16384, 1024], P(('gx', 'gy', 'gz'))
- value_grad: bfloat16 [16384, 1024], P(('gx', 'gy', 'gz'))
Inputs may be any that keep to these rules, and one draw needn't show every extreme that they name: `log_decay`: every entry is negative.
All inputs are finite; a program needn't handle non-finite values.
Results may differ from a plain program's by a relative error of at most 0.0056.
Values sent between devices are 32-bit elements; how exact they have to be, the bound alone decides.
A program may use at most 512 MiB of HBM per device.

v0:
```python
import jax
import jax.numpy as jnp
from jax import lax
from jax.sharding import PartitionSpec as P


def entering(value, axis, join, neutral):
    count, mine = (lax.axis_size(axis), lax.axis_index(axis))
    pieces = jax.tree.map(lambda part: lax.all_gather(part, axis), value)
    pieces = jax.tree.map(lambda part: part[::-1], pieces)
    mine = count - 1 - mine
    subtotal = jax.tree.map(
        lambda part, zero: jnp.full_like(part, 0) + jnp.asarray(zero, part.dtype), value, neutral
    )

    def lap(position, subtotal):
        longer = join(subtotal, jax.tree.map(lambda part: part[position], pieces))
        return jax.tree.map(lambda new, old: jnp.where(position < mine, new, old), longer, subtotal)

    return lax.fori_loop(0, count - 1, lap, subtotal)


def spread(block, axis, source):
    block = jnp.where(lax.axis_index(axis) == source, block, jnp.zeros_like(block))
    return lax.psum(block, axis)


def combine_states(earlier_part, later_part):
    return (
        earlier_part[0] * later_part[0],
        later_part[0][:, None, None] * earlier_part[1] + later_part[1],
    )


def suffix_states(element, identity):
    inner_part = entering(element, "gz", combine_states, identity)
    inner_whole = jax.tree.map(
        lambda part: spread(part, "gz", 0), combine_states(inner_part, element)
    )
    middle_part = entering(inner_whole, "gy", combine_states, identity)
    middle_whole = jax.tree.map(
        lambda part: spread(part, "gy", 0), combine_states(middle_part, inner_whole)
    )
    outer_part = entering(middle_whole, "gx", combine_states, identity)
    return combine_states(combine_states(outer_part, middle_part), inner_part)


def body(queries, keys, values, out_grad, log_decay, saved_states):
    num_heads = log_decay.shape[0]
    count_rows = queries.shape[0]
    head_width = queries.shape[1] // num_heads
    score_scale = head_width ** (-0.5)
    query_heads = queries.reshape(count_rows, num_heads, head_width)
    key_heads = keys.reshape(count_rows, num_heads, head_width)
    value_heads = values.reshape(count_rows, num_heads, head_width)
    grad_heads = out_grad.reshape(count_rows, num_heads, head_width)
    state_in = saved_states[0]
    cumulative = jnp.cumsum(log_decay, axis=1)
    block_end = cumulative[:, -1:]
    to_end = jnp.exp(block_end - cumulative)
    from_start = jnp.exp(cumulative)
    to_end_rows = to_end.T[:, :, None]
    start_rows = (score_scale * from_start).T[:, :, None]
    query_decayed = (query_heads.astype(jnp.float32) * start_rows).astype(jnp.bfloat16)
    local_grad = jnp.einsum(
        "thi,thj->hij", query_decayed, grad_heads, preferred_element_type=jnp.float32
    )
    block_decay = jnp.exp(block_end[:, 0])
    identity = (
        jnp.ones((num_heads,), jnp.float32),
        jnp.zeros((num_heads, head_width, head_width), jnp.float32),
    )
    later_grads = suffix_states((block_decay, local_grad), identity)
    grad_in = later_grads[1].astype(jnp.bfloat16)
    positions = jnp.arange(count_rows, dtype=jnp.int32)
    causal = positions[:, None] >= positions[None, :]
    log_gaps = cumulative[:, :, None] - cumulative[:, None, :]
    weight = jnp.where(causal[None], jnp.exp(jnp.minimum(log_gaps, 0.0)), 0.0)
    probs = (
        jnp.einsum("thd,shd->hts", query_heads, key_heads, preferred_element_type=jnp.float32)
        * score_scale
        * weight
    ).astype(jnp.bfloat16)
    grad_scores = (
        jnp.einsum("thd,shd->hts", grad_heads, value_heads, preferred_element_type=jnp.float32)
        * score_scale
        * weight
    ).astype(jnp.bfloat16)
    query_grad = jnp.einsum(
        "hts,shd->thd", grad_scores, key_heads, preferred_element_type=jnp.float32
    )
    query_grad = (
        query_grad
        + jnp.einsum("thj,hij->thi", grad_heads, state_in, preferred_element_type=jnp.float32)
        * start_rows
    )
    key_grad = jnp.einsum(
        "hts,thd->shd", grad_scores, query_heads, preferred_element_type=jnp.float32
    )
    key_grad = (
        key_grad
        + jnp.einsum("thj,hij->thi", value_heads, grad_in, preferred_element_type=jnp.float32)
        * to_end_rows
    )
    value_grad = jnp.einsum("hts,thd->shd", probs, grad_heads, preferred_element_type=jnp.float32)
    value_grad = (
        value_grad
        + jnp.einsum("thi,hij->thj", key_heads, grad_in, preferred_element_type=jnp.float32)
        * to_end_rows
    )
    total_width = num_heads * head_width
    return (
        query_grad.reshape(count_rows, total_width).astype(jnp.bfloat16),
        key_grad.reshape(count_rows, total_width).astype(jnp.bfloat16),
        value_grad.reshape(count_rows, total_width).astype(jnp.bfloat16),
    )


def solution(mesh):
    in_specs = (
        P(("gx", "gy", "gz"), None),
        P(("gx", "gy", "gz"), None),
        P(("gx", "gy", "gz"), None),
        P(("gx", "gy", "gz"), None),
        P(None, ("gx", "gy", "gz")),
        P(("gx", "gy", "gz"), None, None, None),
    )
    out_specs = (
        P(("gx", "gy", "gz"), None),
        P(("gx", "gy", "gz"), None),
        P(("gx", "gy", "gz"), None),
    )
    return jax.shard_map(body, mesh=mesh, in_specs=in_specs, out_specs=out_specs, check_vma=False)
```

profile of v0, /device:TPU:0, one launch (start us, length us, event | category | flops | bytes accessed | tf_op | source)
XLA Modules:
  0.0 273.5 jit_solution(4662188198473161351)
XLA Ops:
  7.2 0.8 reshape.105
  8.0 1.2 reduce-window.6
  9.2 0.2 slice_reduce_fusion
  9.4 0.2 reduce-window.9
  9.7 0.1 copy.55
  9.9 1.5 copy.56
  11.4 1.9 copy.41
  13.3 1.4 fusion.9
  14.8 0.6 dynamic-slice
  16.0 0.1 bitcast_dynamic-update-slice_fusion
  16.1 2.6 all-reduce
  18.8 9.4 %all-gather.11.cloned.1.call-done = f32[8,256,256]{2,1,0:T(8,128)} async-done(((f32[4,256,256]{2,1,0:T(8,128)}), f32[8,256,256]{2,1,0:T(8,128)}) %all-gather.11.cloned.1.call-update) | async-done | bytes 2097168 | tf_op jit(solution)/shard_map/all_gather | solution.py:9
  28.2 2.8 %add_select_fusion = f32[4,256,256]{2,1,0:T(8,128)} fusion(f32[4,256,256]{2,1,0:T(8,128)} %fusion.9, f32[8,256,256]{2,1,0:T(8,128)} %all-gather.11.cloned.1.call-done, f32[4]{0:T(128)S(1)} %get-tuple-element.308, f32[4]{0:T(128)S(1)} %get-tuple-element.307, pred[]{:T(512)S(6)} %lt.46, pred[]{:T(512)S(6)} %eq.8), kind=kLoop, calls=%fused_computation.33 | loop fusion | flops 1310720 | bytes 3145762 | tf_op jit(solution)/shard_map/jit(_where)/select_n | solution.py:24
  31.1 20.7 %all-reduce.5.cloned.1.call-done = f32[4,256,256]{2,1,0:T(8,128)} async-done(((f32[4,256,256]{2,1,0:T(8,128)}), f32[4,256,256]{2,1,0:T(8,128)}) %all-reduce.5.cloned.1.call-update) | async-done | bytes 1048592 | tf_op jit(solution)/shard_map/psum | solution.py:25
  51.8 2.5 psum.28
  54.3 0.6 dynamic-slice.1
  55.5 0.2 dynamic-update-slice.1
  55.8 12.1 %all-reduce.1 = f32[16]{0:T(128)S(1)} all-reduce(f32[16]{0:T(128)S(1)} %dynamic-update-slice.1), channel_id=3, replica_groups=mesh['gx'=4,'gy'=4,'gz'=2] {'gy'}, use_global_device_ids=true, to_apply=%add.1 | all-reduce | flops 16 | bytes 128
  67.8 0.1 reshape.110
  68.0 67.4 %all-gather.13.cloned.1.call-done = f32[16,256,256]{2,1,0:T(8,128)} async-done(((f32[4,256,256]{2,1,0:T(8,128)}), f32[16,256,256]{2,1,0:T(8,128)}) %all-gather.13.cloned.1.call-update) | async-done | bytes 4194320 | tf_op jit(solution)/shard_map/all_gather | solution.py:9
  135.3 4.6 %rev.15 = f32[4,4,256,256]{3,2,1,0:T(8,128)} reverse(f32[4,4,256,256]{3,2,1,0:T(8,128)} %bitcast.112), dimensions={0} | reverse | bytes 8388608 | tf_op jit(solution)/shard_map/rev | solution.py:10
  139.9 4.9 %while.36 = (s32[]{:T(128)}, f32[4]{0:T(128)S(1)}, f32[4,256,256]{2,1,0:T(8,128)S(1)}, s32[]{:T(128)}, f32[4,4]{1,0:T(4,128)S(1)}, /*index=5*/f32[4,4,256,256]{3,2,1,0:T(8,128)}, s32[]{:T(128)}, s32[]{:T(128)}) while((s32[]{:T(128)}, f32[4]{0:T(128)S(1)}, f32[4,256,256]{2,1,0:T(8,128)S(1)}, s32[]{:T(128)}, f32[4,4]{1,0:T(4,128)S(1)}, ...), condition=%wide.region_5.6_spmd.clone, body=%wide.region_4.5_spmd.clone.sunk | while | flops 1048592 | bytes 3145923 | solution.py:20
  139.9 1.7 fusion.42
  141.6 1.6 fusion.42
  143.2 1.6 fusion.42
  144.8 1.2 select_bitcast_fusion
  146.1 50.5 %all-reduce.7.cloned.1.call-done = f32[1,4,256,256]{3,2,1,0:T(8,128)} async-done(((f32[1,4,256,256]{3,2,1,0:T(8,128)}), f32[1,4,256,256]{3,2,1,0:T(8,128)}) %all-reduce.7.cloned.1.call-update) | async-done | bytes 1048592 | tf_op jit(solution)/shard_map/psum | solution.py:25
  196.7 3.5 %multiply_convert_fusion.1 = bf16[4,512,512]{2,1,0:T(8,128)(2,1)S(1)} fusion(bf16[512,4,256]{0,2,1:T(8,128)(2,1)} %bitcast.109, f32[4,512]{1,0:T(4,128)S(1)} %bitcast.122, pred[512,512]{1,0:T(8,128)(4,1)S(1)} %iota_compare_fusion, bf16[64,4,8,256]{3,2,1,0:T(8,128)(2,1)} %bitcast.119), kind=kOutput, calls=%fused_computation.9 | convolution fusion | flops 543162368 | bytes 4464640 | tf_op jit(solution)/shard_map/thd,shd->hts/dot_general | solution.py:85
  200.3 0.8 fusion.10
  201.0 0.4 copy-done.4
  201.5 1.4 fusion.7
  202.9 2.0 fusion.29
  204.9 5.6 %fusion.8 = f32[4,512,256]{1,2,0:T(8,128)} fusion(bf16[512,4,256]{0,2,1:T(8,128)(2,1)} %bitcast.110, bf16[512,4,256]{0,2,1:T(8,128)(2,1)} %bitcast.106, f32[4,512]{1,0:T(4,128)S(1)} %bitcast.123, pred[512,512]{1,0:T(8,128)(4,1)S(1)} %iota_compare_fusion, bf16[64,4,8,256]{3,2,1,0:T(8,128)(2,1)} %bitcast.113), kind=kOutput, calls=%fused_computation.21 | convolution fusion | flops 1080033280 | bytes 5513216 | tf_op jit(solution)/shard_map/hts,thd->shd/dot_general | solution.py:105
  210.5 2.3 copy.50
  212.8 10.1 %psum.30 = f32[1,4]{1,0:T(1,128)S(1)} all-reduce(f32[1,4]{1,0:T(1,128)S(1)} %fusion.26), channel_id=1, replica_groups=mesh['gx'=4,'gy'=4,'gz'=2] {'gy'}, use_global_device_ids=true, to_apply=%region_6.7 | all-reduce | flops 4 | bytes 32 | tf_op jit(solution)/shard_map/psum | solution.py:25
  222.9 8.2 %all-gather.4 = f32[4,1,4]{2,1,0:T(1,128)S(1)} all-gather(f32[1,1,4]{2,1,0:T(1,128)S(1)} %bitcast.127), channel_id=1, replica_groups=mesh['gx'=4,'gy'=4,'gz'=2] {'gx'}, dimensions={0}, use_global_device_ids=true | all-gather | bytes 80 | tf_op jit(solution)/shard_map/all_gather | solution.py:9
  231.2 19.0 %all-gather.9.cloned.1.call-done = f32[4,4,256,256]{3,2,1,0:T(8,128)} async-done(((f32[1,4,256,256]{3,2,1,0:T(8,128)}), f32[4,4,256,256]{3,2,1,0:T(8,128)}) %all-gather.9.cloned.1.call-update) | async-done | bytes 4194320 | tf_op jit(solution)/shard_map/all_gather | solution.py:9
  250.1 4.5 %rev.17 = f32[4,4,256,256]{3,2,1,0:T(8,128)} reverse(f32[4,4,256,256]{3,2,1,0:T(8,128)} %all-gather.9.cloned.1.call-done), dimensions={0} | reverse | bytes 8388608 | tf_op jit(solution)/shard_map/rev | solution.py:10
  254.6 4.8 %while.37 = (s32[]{:T(128)}, f32[4,256,256]{2,1,0:T(8,128)S(1)}, s32[]{:T(128)}, f32[4,4]{1,0:T(4,128)S(1)}, f32[4,4,256,256]{3,2,1,0:T(8,128)}, /*index=5*/s32[]{:T(128)}, s32[]{:T(128)}) while((s32[]{:T(128)}, f32[4,256,256]{2,1,0:T(8,128)S(1)}, s32[]{:T(128)}, f32[4,4]{1,0:T(4,128)S(1)}, f32[4,4,256,256]{3,2,1,0:T(8,128)}, ...), condition=%wide.region_9.10_spmd.clone, body=%wide.region_8.9_spmd.clone.sunk | while | flops 1048580 | bytes 3145881 | solution.py:20
  254.7 1.6 fusion.43
  256.3 1.6 fusion.43
  257.9 1.6 fusion.43
  259.5 1.7 add_convert_fusion
  261.2 0.5 copy-done.8
  261.7 0.6 fusion.3
  262.3 1.3 copy.52
  263.6 2.1 fusion.5
  265.7 1.3 copy.51
  (52 shorter events, 0.9 us)
Async XLA Ops:
  7.2 193.9 %copy-start = (bf16[1,4,256,256]{3,2,1,0:T(8,128)(2,1)S(1)}, bf16[1,4,256,256]{3,2,1,0:T(8,128)(2,1)}, u32[]{:S(2)}) copy-start(bf16[1,4,256,256]{3,2,1,0:T(8,128)(2,1)} %param.15) | copy-start | bytes 1572868
  7.2 21.0 %all-gather.11.cloned.1.call-start = ((), (), s32[]{:S(2)}) async-start(), calls=%async_computation.3 | async-start | bytes 3145728 | tf_op jit(solution)/shard_map/all_gather | solution.py:9
  11.4 3.4 %copy-start.3 = (bf16[512,1024]{0,1:T(8,128)(2,1)}, bf16[512,1024]{0,1:T(8,128)(2,1)S(1)}, u32[]{:S(2)}) copy-start(bf16[512,1024]{0,1:T(8,128)(2,1)S(1)} %copy.56) | copy-start | bytes 3145732
  13.3 1.5 copy-start.1
  13.3 1.6 copy-start.11
  14.8 37.0 %all-reduce.5.cloned.1.call-start = ((), (), s32[]{:S(2)}) async-start(), calls=%async_computation | async-start | bytes 2097152 | tf_op jit(solution)/shard_map/psum | solution.py:25
  28.2 26.1 %copy-start.10 = (u32[32]{0:T(128)S(1)}, u32[32]{0:T(128)}, u32[]{:S(2)}) copy-start(u32[32]{0:T(128)} %constant.90) | copy-start | bytes 388
  31.0 104.3 %all-gather.13.cloned.1.call-start = ((), (), s32[]{:S(2)}) async-start(), calls=%async_computation.4 | async-start | bytes 5242880 | tf_op jit(solution)/shard_map/all_gather | solution.py:9
  51.8 144.8 %all-reduce.7.cloned.1.call-start = ((), (), s32[]{:S(2)}) async-start(), calls=%async_computation.1 | async-start | bytes 2097152 | tf_op jit(solution)/shard_map/psum | solution.py:25
  139.9 4.9 %copy-start.7 = (f32[4,256,256]{2,1,0:T(8,128)S(1)}, f32[4,256,256]{2,1,0:T(8,128)}, u32[]{:S(2)}) copy-start(f32[4,256,256]{2,1,0:T(8,128)} %all-reduce.5.cloned.1.call-done) | copy-start | bytes 3145732
  146.0 104.1 %all-gather.9.cloned.1.call-start = ((), (), s32[]{:S(2)}) async-start(), calls=%async_computation.2 | async-start | bytes 5242880 | tf_op jit(solution)/shard_map/all_gather | solution.py:9
  196.7 3.6 %copy-start.5 = (bf16[512,1024]{1,0:T(8,128)(2,1)S(1)}, bf16[512,1024]{1,0:T(8,128)(2,1)}, u32[]{:S(2)}) copy-start(bf16[512,1024]{1,0:T(8,128)(2,1)} %param.11) | copy-start | bytes 3145732
  200.2 1.2 copy-start.4
  201.5 1.4 copy-start.2
  259.4 1.7 copy-start.6
  259.5 2.2 copy-start.8
  262.3 1.3 copy-start.9
Sparse Core Ops, SparseCore 0:
  14.9 13.2 all-gather.10
  31.1 20.5 all-reduce.4
  53.3 81.9 all-gather.12
  146.2 50.3 all-reduce.6
  198.3 51.8 all-gather.8
where the time goes:
time: 274 us
  waiting for transfers between devices  167 us (61%)
  blocking collectives  35.5 us (13%)
  local copies, waits for them, and re-layouts  21.2 us (8%)
  matrix products  17.4 us (6%)
  other arithmetic  16.8 us (6%)
  between operations  15.2 us (6%)
    all_gather x3, waiting for transfers between devices, entering(): pieces = jax.tree.map(lambda part: lax.all_gather(part, axis), value)  95.8 us
    psum x2, waiting for transfers between devices, spread(): return lax.psum(block, axis)  71.2 us
    unnamed x2, blocking collectives  14.7 us
    psum x2, blocking collectives, spread(): return lax.psum(block, axis)  12.6 us
    select_n x9, other arithmetic, lap(): jnp.where(position < mine, new, old)  9.53 us
    unnamed x36, local copies, waits for them, and re-layouts  9.45 us
    rev x4, local copies, waits for them, and re-layouts, entering(): pieces = jax.tree.map(lambda part: part[::-1], pieces)  9.13 us
    all_gather x1, blocking collectives, entering(): pieces = jax.tree.map(lambda part: lax.all_gather(part, axis), value)  8.2 us
  transfers between devices with their start and end apart: 5, of which 5 were waited for; matrix products, arithmetic and copies ran while one was open for 6% of the time, Pallas kernels for 0%

commit v1 on v0

v1 whole, which is shorter than its diff:
```python
import functools

import jax
import jax.numpy as jnp
from jax import lax
from jax.experimental import pallas as pl
from jax.experimental.pallas import tpu as pltpu
from jax.sharding import PartitionSpec as P

MESH = pl.DeviceIdType.MESH
F32 = jnp.float32
BF16 = jnp.bfloat16
CHUNKS = 8
DELAY = 2
TILE = 256
NT = (((1,), (1,)), ((), ()))
TN = (((0,), (0,)), ((), ()))
NN = (((1,), (0,)), ((), ()))
LX, FA, FB, RU, RD, FF, FX = 0, 2, 4, 6, 8, 10, 12


def dot(a, b, dims):
    return lax.dot_general(a, b, dims, preferred_element_type=F32)


def kernel(
    sizes, line, steps,
    q_hbm, k_hbm, v_hbm, g_hbm, ld_ref, st_hbm,
    dq_hbm, dk_hbm, dv_hbm,
    q, k, v, g, st, dq, dk, dv, dkacc, dvacc,
    brow, bcol, bend, dvm, gin,
    rbuf, rdec, lsend, ldec, lone, lown, sbuf, done_dec, dchip, tbuf, tdec, xs, xdec, oafter, obuf, gsend, fs,
    in_sem, out_sem, send_sem, recv_sem, dsend_sem, drecv_sem,
):
    gx, gy, gz = sizes
    rows_n, width = q.shape
    heads = ld_ref.shape[0]
    hd = width // heads
    scale = hd ** (-0.5)
    mid = line // 2
    rc = hd // CHUNKS

    lin = (lax.axis_index("gx") * gy + lax.axis_index("gy")) * gz + lax.axis_index("gz")
    core = lin % 2
    chip = lin // 2
    p = chip % line
    col = chip // line

    def dev(core_, p_, col_):
        at = (col_ * line + p_) * 2 + core_
        return (at // (gy * gz), (at // gz) % gy, at % gz)

    def column_partner(s):
        bit = (col // (2**s)) % 2
        return col + (1 - 2 * bit) * (2**s)

    partner = dev(1 - core, p, col)
    up = dev(core, jnp.minimum(p + 1, line - 1), col)
    down = dev(core, jnp.maximum(p - 1, 0), col)
    across = [dev(core, p, column_partner(s)) for s in range(steps)]

    loads = [
        pltpu.make_async_copy(a, b, in_sem.at[n])
        for n, (a, b) in enumerate(
            [(q_hbm, q), (g_hbm, g), (k_hbm, k), (v_hbm, v), (st_hbm.at[0], st)]
        )
    ]
    for load in loads:
        load.start()

    barrier = pltpu.get_barrier_semaphore()

    def greet(to):
        pl.semaphore_signal(barrier, inc=1, device_id=to, device_id_type=MESH)

    greet(partner)
    for s in range(steps):
        greet(across[s])

    @pl.when(p > 0)
    def _():
        greet(down)

    @pl.when(p < line - 1)
    def _():
        greet(up)

    x = ld_ref[...]
    x = jnp.concatenate([x] * (8 // heads), axis=0)
    lane = lax.broadcasted_iota(jnp.int32, x.shape, 1)
    shift = 1
    while shift < rows_n:
        x = x + jnp.where(lane >= shift, pltpu.roll(x, shift, 1), 0.0)
        shift *= 2
    columns = x.T
    end = x[:, rows_n - 1 :]
    for h in range(heads):
        bcol[h] = jnp.broadcast_to(columns[:, h : h + 1], (rows_n, 128))
        bend[h] = jnp.broadcast_to(end[h : h + 1, :], (8, 128))
        brow[h] = jnp.broadcast_to(x[h : h + 1, :], (8, rows_n))
        dvm[h] = jnp.broadcast_to(jnp.exp(end[h : h + 1, :]), (8, hd))

    def wide(a):
        return jnp.concatenate([a] * (hd // 128), axis=1)

    def cols(h):
        return pl.ds(pl.multiple_of(h * hd, hd), hd)

    def local(h):
        start = wide(scale * jnp.exp(bcol[h]))
        decayed = (q[:, cols(h)].astype(F32) * start).astype(BF16)
        return dot(decayed, g[:, cols(h)], TN)

    def decay_of(h):
        return dvm[h]

    def rows(c):
        return pl.ds(pl.multiple_of(c * rc, rc), rc)

    def chunk_copy(src, flow, c, to):
        return pltpu.make_async_remote_copy(
            src_ref=src.at[rows(c)], dst_ref=rbuf.at[flow, rows(c)],
            send_sem=send_sem.at[flow, c], recv_sem=recv_sem.at[flow, c],
            device_id=to, device_id_type=MESH,
        )

    def decay_copy(src, flow, to):
        return pltpu.make_async_remote_copy(
            src_ref=src, dst_ref=rdec.at[flow],
            send_sem=dsend_sem.at[flow], recv_sem=drecv_sem.at[flow],
            device_id=to, device_id_type=MESH,
        )

    def head_copy(src, flow, to):
        return pltpu.make_async_remote_copy(
            src_ref=src, dst_ref=rbuf.at[flow],
            send_sem=send_sem.at[flow, 0], recv_sem=recv_sem.at[flow, 0],
            device_id=to, device_id_type=MESH,
        )

    def send(src, flow, c, to, dec=None):
        if dec is not None:

            @pl.when(c == 0)
            def _():
                decay_copy(dec, flow, to).start()

        chunk_copy(src, flow, c, to).start()

    def recv(flow, c, dec=False):
        if dec:

            @pl.when(c == 0)
            def _():
                decay_copy(rdec.at[flow], flow, partner).wait_recv()

        chunk_copy(rbuf.at[flow], flow, c, partner).wait_recv()

    loads[0].wait()
    loads[1].wait()
    for j in range(2):
        other = 2 * (1 - core) + j
        lsend[j] = local(other)
        ldec[j] = decay_of(other)
        if j == 0:
            ends = (p > 0).astype(jnp.int32) + (p < line - 1).astype(jnp.int32)
            pl.semaphore_wait(barrier, 1 + steps + ends)

        decay_copy(ldec.at[j], LX + j, partner).start()
        head_copy(lsend.at[j], LX + j, partner).start()
    for j in range(2):
        lown[j] = local(2 * core + j)
    for j in range(2):
        mine = decay_of(2 * core + j)
        decay_copy(ldec.at[j], LX + j, partner).wait_recv()
        head_copy(lsend.at[j], LX + j, partner).wait_recv()
        theirs = rdec[LX + j]
        dchip[j] = mine * theirs

        @pl.when(core == 0)
        def _():
            lone[j] = rbuf[LX + j]
            sbuf[j] = lown[j] + mine[:1] * rbuf[LX + j]
            done_dec[j] = theirs

        @pl.when(core == 1)
        def _():
            lone[j] = lown[j]
            sbuf[j] = rbuf[LX + j] + theirs[:1] * lown[j]
            done_dec[j] = mine

    for load in loads[2:]:
        load.wait()

    tiles = rows_n // TILE

    def block(h, r):
        hs = cols(h)
        at = slice(r * TILE, (r + 1) * TILE)
        extent = (r + 1) * TILE
        qt, gt = q[at, hs], g[at, hs]
        ks, vs = k[:extent, hs], v[:extent, hs]
        bt = bcol[h, at, :]
        weights = []
        for n in range(extent // 128):
            gap = bt - brow[h, :1, pl.ds(n * 128, 128)]
            weight = jnp.exp(jnp.minimum(gap, 0.0))
            if (n + 1) * 128 > r * TILE:
                ti = lax.broadcasted_iota(jnp.int32, gap.shape, 0) + r * TILE
                si = lax.broadcasted_iota(jnp.int32, gap.shape, 1) + n * 128
                weight = jnp.where(ti >= si, weight, 0.0)
            weights.append(weight)
        weight = jnp.concatenate(weights, axis=1)
        probs = (dot(qt, ks, NT) * scale * weight).astype(BF16)
        gscores = (dot(gt, vs, NT) * scale * weight).astype(BF16)
        start = wide(scale * jnp.exp(bt))
        dqt = dot(gscores, ks, NN) + dot(gt, st[h], NT) * start
        dq[at, hs] = dqt.astype(BF16)
        dkp = dot(gscores, qt, TN)
        dvp = dot(probs, gt, TN)
        if r:
            dkacc[: r * TILE, hs] += dkp[: r * TILE]
            dvacc[: r * TILE, hs] += dvp[: r * TILE]
        dkacc[at, hs] = dkp[r * TILE :]
        dvacc[at, hs] = dvp[r * TILE :]

    def finish(j, c, grad):
        at = rows(c)
        alt = lone[j, at] + done_dec[j, :1] * grad
        first = core == 0
        gin[2 * core + j, at] = jnp.where(first, alt, grad).astype(BF16)
        fs[j, at] = jnp.where(first, grad, alt)
        send(fs.at[j], FF + j, c, partner)

    def step(t, carry):
        for j in range(2):
            own = mid - 1 + j

            c = t - DELAY * (mid + steps + jnp.abs(p - own))
            ok = (c >= 0) & (c < CHUNKS)

            @pl.when(ok & (p > own))
            def _():
                recv(RU + j, c)
                at = rows(c)

                @pl.when(p < line - 1)
                def _():
                    send(rbuf.at[RU + j], RU + j, c, up)
                    finish(j, c, rbuf[FA + j, at] + rdec[FA + j, :1] * rbuf[RU + j, at])

                @pl.when(p == line - 1)
                def _():
                    finish(j, c, rbuf[RU + j, at])

            @pl.when(ok & (p < own))
            def _():
                recv(RD + j, c)
                at = rows(c)

                @pl.when(p > 0)
                def _():
                    gsend[j, at] = sbuf[j, at] + dchip[j, :1] * rbuf[RD + j, at]
                    send(gsend.at[j], RD + j, c, down)

                finish(j, c, rbuf[RD + j, at])

            for s in reversed(range(steps)):
                c = t - DELAY * (mid + 1 + s)

                @pl.when((c >= 0) & (c < CHUNKS) & (p == own))
                def _():
                    recv(FX + s, c, True)
                    at = rows(c)
                    later = (col // (2**s)) % 2 == 0

                    @pl.when(c == 0)
                    def _():
                        oafter[s + 1] = jnp.where(later, oafter[s] * rdec[FX + s], oafter[s])
                        if s < steps - 1:
                            xdec[s + 1] = xdec[s] * rdec[FX + s]

                    theirs, mine = rbuf[FX + s, at], xs[s, at]
                    total = obuf[at] + jnp.where(later, oafter[s, :1] * theirs, 0.0)
                    obuf[at] = total
                    if s < steps - 1:
                        xs[s + 1, at] = jnp.where(
                            later, mine + xdec[s, :1] * theirs, theirs + rdec[FX + s, :1] * mine
                        )
                        send(xs.at[s + 1], FX + s + 1, c, across[s + 1], xdec.at[s + 1])
                    else:
                        send(obuf, RU + j, c, up)
                        grad = rbuf[FA + j, at] + rdec[FA + j, :1] * total
                        gsend[j, at] = sbuf[j, at] + dchip[j, :1] * grad
                        send(gsend.at[j], RD + j, c, down)
                        finish(j, c, grad)

            stage = jnp.where(p > own, line - 1 - p, jnp.where(p < own, p, mid))
            c = t - DELAY * stage
            ok = (c >= 0) & (c < CHUNKS)

            @pl.when(ok & (p > own))
            def _():
                at = rows(c)

                @pl.when(p < line - 1)
                def _():
                    recv(FA + j, c, True)

                    @pl.when(c == 0)
                    def _():
                        tdec[j] = dchip[j] * rdec[FA + j]

                    tbuf[j, at] = sbuf[j, at] + dchip[j, :1] * rbuf[FA + j, at]

                @pl.when(p == line - 1)
                def _():
                    @pl.when(c == 0)
                    def _():
                        tdec[j] = dchip[j]

                    tbuf[j, at] = sbuf[j, at]

                send(tbuf.at[j], FA + j, c, down, tdec.at[j])

            @pl.when(ok & (p < own))
            def _():
                at = rows(c)

                @pl.when(p > 0)
                def _():
                    recv(FB + j, c, True)

                    @pl.when(c == 0)
                    def _():
                        tdec[j] = dchip[j] * rdec[FB + j]

                    tbuf[j, at] = rbuf[FB + j, at] + rdec[FB + j, :1] * sbuf[j, at]

                @pl.when(p == 0)
                def _():
                    @pl.when(c == 0)
                    def _():
                        tdec[j] = dchip[j]

                    tbuf[j, at] = sbuf[j, at]

                send(tbuf.at[j], FB + j, c, up, tdec.at[j])

            @pl.when(ok & (p == own))
            def _():
                at = rows(c)
                recv(FA + j, c, True)
                recv(FB + j, c, True)

                @pl.when(c == 0)
                def _():
                    xdec[0] = rdec[FB + j] * dchip[j] * rdec[FA + j]
                    oafter[0] = jnp.ones_like(oafter[0])

                whole = sbuf[j, at] + dchip[j, :1] * rbuf[FA + j, at]
                xs[0, at] = rbuf[FB + j, at] + rdec[FB + j, :1] * whole
                obuf[at] = jnp.zeros((rc, hd), F32)
                send(xs.at[0], FX, c, across[0], xdec.at[0])

        for r in range(tiles):

            @pl.when((t < heads * tiles) & (t % tiles == r))
            def _():
                block(t // tiles, r)

        return carry

    last = CHUNKS + DELAY * (mid + steps + mid)
    lax.fori_loop(0, max(last, heads * tiles), step, 0)

    outs = [pltpu.make_async_copy(dq, dq_hbm, out_sem.at[0])]
    outs[0].start()

    def final(n, h):
        hs = cols(h)
        to_end = wide(jnp.exp(bend[h, :1] - bcol[h]))
        dk[:, hs] = (dkacc[:, hs] + dot(v[:, hs], gin[h], NT) * to_end).astype(BF16)
        outs.append(pltpu.make_async_copy(dk.at[:, hs], dk_hbm.at[:, hs], out_sem.at[1 + 2 * n]))
        outs[-1].start()
        dv[:, hs] = (dvacc[:, hs] + dot(k[:, hs], gin[h], NN) * to_end).astype(BF16)
        outs.append(pltpu.make_async_copy(dv.at[:, hs], dv_hbm.at[:, hs], out_sem.at[2 + 2 * n]))
        outs[-1].start()

    for j in range(2):
        final(j, 2 * core + j)
    for j in range(2):
        for c in range(CHUNKS):
            recv(FF + j, c)
        gin[2 * (1 - core) + j] = rbuf[FF + j].astype(BF16)
        final(2 + j, 2 * (1 - core) + j)

    def sent(flow, src, dec=None):
        if dec is not None:
            decay_copy(dec, flow, partner).wait_send()
        for c in range(CHUNKS):
            chunk_copy(src, flow, c, partner).wait_send()

    for j in range(2):
        own = mid - 1 + j
        decay_copy(ldec.at[j], LX + j, partner).wait_send()
        head_copy(lsend.at[j], LX + j, partner).wait_send()
        sent(FF + j, fs.at[j])

        @pl.when(p > own)
        def _():
            sent(FA + j, tbuf.at[j], tdec.at[j])

        @pl.when(p < own)
        def _():
            sent(FB + j, tbuf.at[j], tdec.at[j])

        @pl.when((p >= own) & (p < line - 1))
        def _():
            sent(RU + j, obuf)

        @pl.when((p <= own) & (p > 0))
        def _():
            sent(RD + j, gsend.at[j])

        @pl.when(p == own)
        def _():
            for s in range(steps):
                sent(FX + s, xs.at[s], xdec.at[s])

    for out in outs:
        out.wait()


def solution(mesh):
    sizes = tuple(mesh.shape[a] for a in ("gx", "gy", "gz"))
    gx, gy, gz = sizes
    line = gz // 2 if gz > 2 else gy
    columns = gx * gy * gz // (2 * line)
    steps = columns.bit_length() - 1
    assert line % 2 == 0 and line >= 4 and columns == 2**steps and steps >= 1

    def body(queries, keys, values, out_grad, log_decay, saved_states):
        n, width = queries.shape
        heads = log_decay.shape[0]
        hd = width // heads
        assert heads == 4
        flows = FX + steps
        any_ = pl.BlockSpec(memory_space=pl.ANY)
        hbm = pl.BlockSpec(memory_space=pltpu.HBM)
        state = (hd, hd)
        tile = (8, hd)
        out = jax.ShapeDtypeStruct((n, width), BF16)
        vm = pltpu.VMEM
        return pl.pallas_call(
            functools.partial(kernel, sizes, line, steps),
            out_shape=(out, out, out),
            in_specs=[hbm] * 4 + [pl.BlockSpec(memory_space=pltpu.VMEM), hbm],
            out_specs=(any_,) * 3,
            scratch_shapes=[
                vm((n, width), BF16), vm((n, width), BF16), vm((n, width), BF16), vm((n, width), BF16),
                vm((heads,) + state, BF16),
                vm((n, width), BF16), vm((n, width), BF16), vm((n, width), BF16),
                vm((n, width), F32), vm((n, width), F32),
                vm((heads, 8, n), F32), vm((heads, n, 128), F32), vm((heads, 8, 128), F32), vm((heads,) + tile, F32),
                vm((heads,) + state, BF16),
                vm((flows,) + state, F32), vm((flows,) + tile, F32),
                vm((2,) + state, F32), vm((2,) + tile, F32),
                vm((2,) + state, F32), vm((2,) + state, F32), vm((2,) + state, F32),
                vm((2,) + tile, F32), vm((2,) + tile, F32),
                vm((2,) + state, F32), vm((2,) + tile, F32),
                vm((steps,) + state, F32), vm((steps,) + tile, F32), vm((steps + 1,) + tile, F32),
                vm(state, F32), vm((2,) + state, F32), vm((2,) + state, F32),
                pltpu.SemaphoreType.DMA((5,)), pltpu.SemaphoreType.DMA((1 + 2 * heads,)),
                pltpu.SemaphoreType.DMA((flows, CHUNKS)), pltpu.SemaphoreType.DMA((flows, CHUNKS)),
                pltpu.SemaphoreType.DMA((flows,)), pltpu.SemaphoreType.DMA((flows,)),
            ],
            compiler_params=pltpu.CompilerParams(
                collective_id=0, has_side_effects=True, vmem_limit_bytes=60 * 1024 * 1024
            ),
        )(queries, keys, values, out_grad, log_decay, saved_states)

    seq = ("gx", "gy", "gz")
    return jax.shard_map(
        body,
        mesh=mesh,
        in_specs=(P(seq, None),) * 4 + (P(None, seq), P(seq, None, None, None)),
        out_specs=(P(seq, None),) * 3,
        check_vma=False,
    )
```

time: 274 us -> 47.4 us (0.17)
  waiting for transfers between devices: 167 us -> 0 us
  Pallas kernels: 0 us -> 41.6 us
  blocking collectives: 35.5 us -> 0 us
  matrix products: 17.4 us -> 0 us
  other arithmetic: 16.8 us -> 0 us
  local copies, waits for them, and re-layouts: 21.2 us -> 4.93 us
  between operations: 15.2 us -> 0.65 us
    all_gather x3 -> x0, waiting for transfers between devices: 95.8 us -> none  [entering(): pieces = jax.tree.map(lambda part: lax.all_gather(part, axis), value)]
    psum x2 -> x0, waiting for transfers between devices: 71.2 us -> none  [spread(): return lax.psum(block, axis)]
    pallas_call x0 -> x1, Pallas kernels: none -> 41.6 us  [body(): pl.pallas_call(functools.partial(kernel, sizes, line, steps), out_shape=(...]
    dot_general x8 -> x0, matrix products: 17.4 us -> none  [the longest x1 5.59 us: body(): jnp.einsum('hts,thd->shd', probs, grad_heads, preferred_element_type=jnp....]
    unnamed x2 -> x0, blocking collectives: 14.7 us -> none
    psum x2 -> x0, blocking collectives: 12.6 us -> none  [spread(): return lax.psum(block, axis)]
    select_n x11 -> x0, other arithmetic: 12.4 us -> none  [the longest x9 9.53 us: lap(): jnp.where(position < mine, new, old)]
    rev x4 -> x0, local copies, waits for them, and re-layouts: 9.13 us -> none  [entering(): pieces = jax.tree.map(lambda part: part[::-1], pieces)]
  transfers between devices with their start and end apart: 5 -> 0, of which waited for: 5 -> 0; matrix products, arithmetic and copies ran while one was open for 6% -> 0% of each run, Pallas kernels for 0% -> 0%
where the time goes in v1:
time: 47.4 us; the launch traced here: 47.1 us
  Pallas kernels  41.6 us (88%)
  local copies, waits for them, and re-layouts  4.93 us (10%)
  between operations  0.65 us (1%)
    pallas_call x1, Pallas kernels, body(): pl.pallas_call(functools.partial(kernel, sizes, line, steps), out_shape=(...  41.6 us
    unnamed x7, local copies, waits for them, and re-layouts  4.93 us

profile of v1, /device:TPU:0, one launch (start us, length us, event | category | flops | bytes accessed | tf_op | source)
XLA Modules:
  0.0 47.1 jit_solution(6783078714872832093)
XLA Ops:
  0.6 41.6 %shard_map.85 = (bf16[512,1024]{1,0:T(8,128)(2,1)}, bf16[512,1024]{1,0:T(8,128)(2,1)}, bf16[512,1024]{1,0:T(8,128)(2,1)}) custom-call(bf16[512,1024]{1,0:T(8,128)(2,1)} %q_hbm.1, bf16[512,1024]{1,0:T(8,128)(2,1)} %k_hbm.1, bf16[512,1024]{1,0:T(8,128)(2,1)} %v_hbm.1, bf16[512,1024]{1,0:T(8,128)(2,1)} %g_hbm.1, f32[4,512]{1,0:T(4,128)} %ld_ref.1, ...), custom_call_target="tpu_custom_call" | custom-call | tf_op jit(solution)/shard_map/pallas_call | solution.py:455
  42.2 0.0 copy-start.1
  42.2 2.4 %copy.12 = bf16[512,1024]{1,0:T(8,128)(2,1)} copy(bf16[512,1024]{1,0:T(8,128)(2,1)} %get-tuple-element.6) | data formatting | bytes 2097152
  44.6 0.0 copy-done.1
  44.6 0.0 copy-start
  44.6 1.0 %copy.13 = bf16[512,1024]{1,0:T(8,128)(2,1)} copy(bf16[512,1024]{1,0:T(8,128)(2,1)S(1)} %copy-done.1) | data formatting | bytes 2097152
  45.5 0.6 %copy-done = bf16[512,1024]{1,0:T(8,128)(2,1)S(1)} copy-done((bf16[512,1024]{1,0:T(8,128)(2,1)S(1)}, bf16[512,1024]{1,0:T(8,128)(2,1)}, u32[]{:S(2)}) %copy-start) | copy-done | bytes 1048600
  46.2 1.0 %copy.14 = bf16[512,1024]{1,0:T(8,128)(2,1)} copy(bf16[512,1024]{1,0:T(8,128)(2,1)S(1)} %copy-done) | data formatting | bytes 2097152
Async XLA Ops:
  42.2 2.4 %copy-start.1 = (bf16[512,1024]{1,0:T(8,128)(2,1)S(1)}, bf16[512,1024]{1,0:T(8,128)(2,1)}, u32[]{:S(2)}) copy-start(bf16[512,1024]{1,0:T(8,128)(2,1)} %get-tuple-element.7) | copy-start | bytes 3145732
  44.6 1.6 %copy-start = (bf16[512,1024]{1,0:T(8,128)(2,1)S(1)}, bf16[512,1024]{1,0:T(8,128)(2,1)}, u32[]{:S(2)}) copy-start(bf16[512,1024]{1,0:T(8,128)(2,1)} %get-tuple-element.8) | copy-start | bytes 3145732

commit v2 on v1

v2 whole, which is shorter than its diff:
```python
import functools

import jax
import jax.numpy as jnp
from jax import lax
from jax.experimental import pallas as pl
from jax.experimental.pallas import tpu as pltpu
from jax.sharding import PartitionSpec as P

MESH = pl.DeviceIdType.MESH
F32 = jnp.float32
BF16 = jnp.bfloat16
PIECES = 4
PER_PIECE = 4
DELAY = 3
TILE = 256
NT = (((1,), (1,)), ((), ()))
TN = (((0,), (0,)), ((), ()))
NN = (((1,), (0,)), ((), ()))
LX, FA, FB, RU, RD, FF, FX = 0, 2, 4, 6, 8, 10, 12
DL, DA, DB, DX = 0, 2, 2 + PIECES, 2 + 2 * PIECES
CHUNKS = PIECES * PER_PIECE // 2


def dot(a, b, dims):
    return lax.dot_general(a, b, dims, preferred_element_type=F32)


def kernel(
    sizes, line, steps,
    q_hbm, k_hbm, v_hbm, g_hbm, ld_ref, st_hbm,
    dq, dk, dv,
    q, k, v, g, st, dkacc, dvacc,
    brow, bcol, bend, dvm, gin,
    rbuf, rdec, lsend, ldec, lone, lown, sbuf, done_dec, dchip, tbuf, tdec, xs, xdec, oafter, obuf, gsend, fs,
    in_sem, send_sem, recv_sem, dsend_sem, drecv_sem,
):
    gx, gy, gz = sizes
    rows_n, width = q.shape
    heads = ld_ref.shape[0]
    hd = width // heads
    scale = hd ** (-0.5)
    rc = hd // CHUNKS

    lin = (lax.axis_index("gx") * gy + lax.axis_index("gy")) * gz + lax.axis_index("gz")
    core = lin % 2
    chip = lin // 2
    p = chip % line
    col = chip // line

    def dev(core_, p_, col_):
        at = (col_ * line + p_) * 2 + core_
        return (at // (gy * gz), (at // gz) % gy, at % gz)

    def column_partner(s):
        bit = (col // (2**s)) % 2
        return col + (1 - 2 * bit) * (2**s)

    partner = dev(1 - core, p, col)
    up = dev(core, jnp.minimum(p + 1, line - 1), col)
    down = dev(core, jnp.maximum(p - 1, 0), col)
    across = [dev(core, p, column_partner(s)) for s in range(steps)]

    loads = [
        pltpu.make_async_copy(a, b, in_sem.at[n])
        for n, (a, b) in enumerate(
            [(q_hbm, q), (g_hbm, g), (k_hbm, k), (v_hbm, v), (st_hbm.at[0], st)]
        )
    ]
    for load in loads:
        load.start()

    barrier = pltpu.get_barrier_semaphore()

    def greet(to):
        pl.semaphore_signal(barrier, inc=1, device_id=to, device_id_type=MESH)

    greet(partner)
    for s in range(steps):
        greet(across[s])

    @pl.when(p > 0)
    def _():
        greet(down)

    @pl.when(p < line - 1)
    def _():
        greet(up)

    x = ld_ref[...]
    x = jnp.concatenate([x] * (8 // heads), axis=0)
    lane = lax.broadcasted_iota(jnp.int32, x.shape, 1)
    shift = 1
    while shift < rows_n:
        x = x + jnp.where(lane >= shift, pltpu.roll(x, shift, 1), 0.0)
        shift *= 2
    columns = x.T
    end = x[:, rows_n - 1 :]
    for h in range(heads):
        bcol[h] = jnp.broadcast_to(columns[:, h : h + 1], (rows_n, 128))
        bend[h] = jnp.broadcast_to(end[h : h + 1, :], (8, 128))
        brow[h] = jnp.broadcast_to(x[h : h + 1, :], (8, rows_n))
        dvm[h] = jnp.broadcast_to(jnp.exp(end[h : h + 1, :]), (8, hd))

    def wide(a):
        return jnp.concatenate([a] * (hd // 128), axis=1)

    def cols(h):
        return pl.ds(pl.multiple_of(h * hd, hd), hd)

    def local(h):
        start = wide(scale * jnp.exp(bcol[h]))
        decayed = (q[:, cols(h)].astype(F32) * start).astype(BF16)
        return dot(decayed, g[:, cols(h)], TN)

    def decay_of(h):
        return dvm[h]

    def rows(c):
        return pl.ds(pl.multiple_of(c * rc, rc), rc)

    def chunk_copy(src, flow, c, to):
        return pltpu.make_async_remote_copy(
            src_ref=src.at[rows(c)], dst_ref=rbuf.at[flow, rows(c)],
            send_sem=send_sem.at[flow, c], recv_sem=recv_sem.at[flow, c],
            device_id=to, device_id_type=MESH,
        )

    def decay_copy(src, flow, to):
        return pltpu.make_async_remote_copy(
            src_ref=src, dst_ref=rdec.at[flow],
            send_sem=dsend_sem.at[flow], recv_sem=drecv_sem.at[flow],
            device_id=to, device_id_type=MESH,
        )

    def head_copy(src, flow, to):
        return pltpu.make_async_remote_copy(
            src_ref=src, dst_ref=rbuf.at[flow],
            send_sem=send_sem.at[flow, 0], recv_sem=recv_sem.at[flow, 0],
            device_id=to, device_id_type=MESH,
        )

    def send(src, flow, c, to):
        chunk_copy(src, flow, c, to).start()

    def recv(flow, c):
        chunk_copy(rbuf.at[flow], flow, c, partner).wait_recv()

    def recv_decay(flow):
        decay_copy(rdec.at[flow], flow, partner).wait_recv()

    loads[0].wait()
    loads[1].wait()
    for j in range(2):
        other = 2 * (1 - core) + j
        lsend[j] = local(other)
        ldec[j] = decay_of(other)
        if j == 0:
            ends = (p > 0).astype(jnp.int32) + (p < line - 1).astype(jnp.int32)
            pl.semaphore_wait(barrier, 1 + steps + ends)

        decay_copy(ldec.at[j], DL + j, partner).start()
        head_copy(lsend.at[j], LX + j, partner).start()
    for j in range(2):
        lown[j] = local(2 * core + j)
    for j in range(2):
        mine = decay_of(2 * core + j)
        decay_copy(ldec.at[j], DL + j, partner).wait_recv()
        head_copy(lsend.at[j], LX + j, partner).wait_recv()
        theirs = rdec[DL + j]
        dchip[j] = mine * theirs

        @pl.when(core == 0)
        def _():
            lone[j] = rbuf[LX + j]
            sbuf[j] = lown[j] + mine[:1] * rbuf[LX + j]
            done_dec[j] = theirs

        @pl.when(core == 1)
        def _():
            lone[j] = lown[j]
            sbuf[j] = rbuf[LX + j] + theirs[:1] * lown[j]
            done_dec[j] = mine

    for load in loads[2:]:
        load.wait()

    tiles = rows_n // TILE

    def block(h, r):
        hs = cols(h)
        at = slice(r * TILE, (r + 1) * TILE)
        extent = (r + 1) * TILE
        qt, gt = q[at, hs], g[at, hs]
        ks, vs = k[:extent, hs], v[:extent, hs]
        bt = bcol[h, at, :]
        weights = []
        for n in range(extent // 128):
            gap = bt - brow[h, :1, pl.ds(n * 128, 128)]
            weight = jnp.exp(jnp.minimum(gap, 0.0))
            if (n + 1) * 128 > r * TILE:
                ti = lax.broadcasted_iota(jnp.int32, gap.shape, 0) + r * TILE
                si = lax.broadcasted_iota(jnp.int32, gap.shape, 1) + n * 128
                weight = jnp.where(ti >= si, weight, 0.0)
            weights.append(weight)
        weight = jnp.concatenate(weights, axis=1)
        probs = (dot(qt, ks, NT) * scale * weight).astype(BF16)
        gscores = (dot(gt, vs, NT) * scale * weight).astype(BF16)
        start = wide(scale * jnp.exp(bt))
        dqt = dot(gscores, ks, NN) + dot(gt, st[h], NT) * start
        dq[at, hs] = dqt.astype(BF16)
        dkp = dot(gscores, qt, TN)
        dvp = dot(probs, gt, TN)
        if r:
            dkacc[: r * TILE, hs] += dkp[: r * TILE]
            dvacc[: r * TILE, hs] += dvp[: r * TILE]
        dkacc[at, hs] = dkp[r * TILE :]
        dvacc[at, hs] = dvp[r * TILE :]

    def finish(j, c, grad):
        at = rows(c)
        alt = lone[j, at] + done_dec[j, :1] * grad
        first = core == 0
        gin[2 * core + j, at] = jnp.where(first, alt, grad).astype(BF16)
        fs[j, at] = jnp.where(first, grad, alt)
        send(fs.at[j], FF + j, c, partner)

    owners = [n * line // PIECES for n in range(PIECES)]
    from_high = [PER_PIECE * n for n in range(PIECES)]
    from_low = [PER_PIECE * (PIECES - 1 - n) for n in range(PIECES)]
    own_at = []
    for n, own in enumerate(owners):
        reach = []
        if own < line - 1:
            reach.append(from_high[n] + DELAY * (line - 1 - own))
        if own > 0:
            reach.append(from_low[n] + DELAY * own)
        own_at.append(max(reach))

    def piece(n, t):
        j, own = n // 2, owners[n]
        base = (n % 2) * PER_PIECE

        def when(start):
            c = t - start
            return c, (c >= 0) & (c < PER_PIECE)

        c, ok = when(own_at[n] + DELAY * (steps + jnp.abs(p - own)))
        cg = base + c
        at = rows(cg)

        if own < line - 1:

            @pl.when(ok & (p > own))
            def _():
                recv(RU + j, cg)

                @pl.when(p < line - 1)
                def _():
                    send(rbuf.at[RU + j], RU + j, cg, up)
                    finish(j, cg, rbuf[FA + j, at] + rdec[DA + n, :1] * rbuf[RU + j, at])

                @pl.when(p == line - 1)
                def _():
                    finish(j, cg, rbuf[RU + j, at])

        if own > 0:

            @pl.when(ok & (p < own))
            def _():
                recv(RD + j, cg)

                @pl.when(p > 0)
                def _():
                    gsend[j, at] = sbuf[j, at] + dchip[j, :1] * rbuf[RD + j, at]
                    send(gsend.at[j], RD + j, cg, down)

                finish(j, cg, rbuf[RD + j, at])

        for s in reversed(range(steps)):
            c, ok = when(own_at[n] + DELAY * (1 + s))

            @pl.when(ok & (p == own))
            def _():
                cg = base + c
                at = rows(cg)
                later = (col // (2**s)) % 2 == 0

                @pl.when(c == 0)
                def _():
                    recv_decay(DX + s)
                    oafter[s + 1] = jnp.where(later, oafter[s] * rdec[DX + s], oafter[s])
                    if s < steps - 1:
                        xdec[s + 1] = xdec[s] * rdec[DX + s]
                        decay_copy(xdec.at[s + 1], DX + s + 1, across[s + 1]).start()

                recv(FX + s, cg)
                theirs, mine = rbuf[FX + s, at], xs[s, at]
                total = obuf[at] + jnp.where(later, oafter[s, :1] * theirs, 0.0)
                obuf[at] = total
                if s < steps - 1:
                    xs[s + 1, at] = jnp.where(
                        later, mine + xdec[s, :1] * theirs, theirs + rdec[DX + s, :1] * mine
                    )
                    send(xs.at[s + 1], FX + s + 1, cg, across[s + 1])
                else:
                    if own < line - 1:
                        send(obuf, RU + j, cg, up)
                        grad = rbuf[FA + j, at] + rdec[DA + n, :1] * total
                    else:
                        grad = total
                    if own > 0:
                        gsend[j, at] = sbuf[j, at] + dchip[j, :1] * grad
                        send(gsend.at[j], RD + j, cg, down)
                    finish(j, cg, grad)

        if own < line - 1:
            c, ok = when(from_high[n] + DELAY * (line - 1 - p))

            @pl.when(ok & (p > own))
            def _():
                cg = base + c
                at = rows(cg)

                @pl.when(p < line - 1)
                def _():
                    @pl.when(c == 0)
                    def _():
                        recv_decay(DA + n)
                        tdec[n] = dchip[j] * rdec[DA + n]

                    recv(FA + j, cg)
                    tbuf[j, at] = sbuf[j, at] + dchip[j, :1] * rbuf[FA + j, at]

                @pl.when(p == line - 1)
                def _():
                    @pl.when(c == 0)
                    def _():
                        tdec[n] = dchip[j]

                    tbuf[j, at] = sbuf[j, at]

                @pl.when(c == 0)
                def _():
                    decay_copy(tdec.at[n], DA + n, down).start()

                send(tbuf.at[j], FA + j, cg, down)

        if own > 0:
            c, ok = when(from_low[n] + DELAY * p)

            @pl.when(ok & (p < own))
            def _():
                cg = base + c
                at = rows(cg)

                @pl.when(p > 0)
                def _():
                    @pl.when(c == 0)
                    def _():
                        recv_decay(DB + n)
                        tdec[n] = dchip[j] * rdec[DB + n]

                    recv(FB + j, cg)
                    tbuf[j, at] = rbuf[FB + j, at] + rdec[DB + n, :1] * sbuf[j, at]

                @pl.when(p == 0)
                def _():
                    @pl.when(c == 0)
                    def _():
                        tdec[n] = dchip[j]

                    tbuf[j, at] = sbuf[j, at]

                @pl.when(c == 0)
                def _():
                    decay_copy(tdec.at[n], DB + n, up).start()

                send(tbuf.at[j], FB + j, cg, up)

        c, ok = when(own_at[n])

        @pl.when(ok & (p == own))
        def _():
            cg = base + c
            at = rows(cg)

            @pl.when(c == 0)
            def _():
                decay = dchip[j]
                if own < line - 1:
                    recv_decay(DA + n)
                    decay = decay * rdec[DA + n]
                if own > 0:
                    recv_decay(DB + n)
                    decay = decay * rdec[DB + n]
                xdec[0] = decay
                oafter[0] = jnp.ones_like(oafter[0])
                decay_copy(xdec.at[0], DX, across[0]).start()

            whole = sbuf[j, at]
            if own < line - 1:
                recv(FA + j, cg)
                whole = whole + dchip[j, :1] * rbuf[FA + j, at]
            if own > 0:
                recv(FB + j, cg)
                whole = rbuf[FB + j, at] + rdec[DB + n, :1] * whole
            xs[0, at] = whole
            obuf[at] = jnp.zeros((rc, hd), F32)
            send(xs.at[0], FX, cg, across[0])

    def step(t, carry):
        for n in range(PIECES):
            piece(n, t)

        for r in range(tiles):

            @pl.when((t < heads * tiles) & (t % tiles == r))
            def _():
                block(t // tiles, r)

        return carry

    last = max(
        own_at[n] + DELAY * (steps + max(own, line - 1 - own)) for n, own in enumerate(owners)
    )
    lax.fori_loop(0, max(last + PER_PIECE, heads * tiles), step, 0)

    def final(h):
        hs = cols(h)
        to_end = wide(jnp.exp(bend[h, :1] - bcol[h]))
        dk[:, hs] = (dkacc[:, hs] + dot(v[:, hs], gin[h], NT) * to_end).astype(BF16)
        dv[:, hs] = (dvacc[:, hs] + dot(k[:, hs], gin[h], NN) * to_end).astype(BF16)

    for j in range(2):
        final(2 * core + j)
    for j in range(2):
        for c in range(CHUNKS):
            recv(FF + j, c)
        gin[2 * (1 - core) + j] = rbuf[FF + j].astype(BF16)
        final(2 * (1 - core) + j)

    def sent(flow, src, base, count):
        for c in range(base, base + count):
            chunk_copy(src, flow, c, partner).wait_send()

    for j in range(2):
        decay_copy(ldec.at[j], DL + j, partner).wait_send()
        head_copy(lsend.at[j], LX + j, partner).wait_send()
        sent(FF + j, fs.at[j], 0, CHUNKS)

    for n, own in enumerate(owners):
        j, base = n // 2, (n % 2) * PER_PIECE

        @pl.when(p > own)
        def _():
            decay_copy(tdec.at[n], DA + n, partner).wait_send()
            sent(FA + j, tbuf.at[j], base, PER_PIECE)

        @pl.when(p < own)
        def _():
            decay_copy(tdec.at[n], DB + n, partner).wait_send()
            sent(FB + j, tbuf.at[j], base, PER_PIECE)

        @pl.when((p >= own) & (p < line - 1))
        def _():
            sent(RU + j, obuf, base, PER_PIECE)

        @pl.when((p <= own) & (p > 0))
        def _():
            sent(RD + j, gsend.at[j], base, PER_PIECE)

        @pl.when(p == own)
        def _():
            for s in range(steps):
                decay_copy(xdec.at[s], DX + s, partner).wait_send()
                sent(FX + s, xs.at[s], base, PER_PIECE)


def solution(mesh):
    sizes = tuple(mesh.shape[a] for a in ("gx", "gy", "gz"))
    gx, gy, gz = sizes
    line = gz // 2 if gz > 2 else gy
    columns = gx * gy * gz // (2 * line)
    steps = columns.bit_length() - 1
    assert line % PIECES == 0 and columns == 2**steps and steps >= 1

    def body(queries, keys, values, out_grad, log_decay, saved_states):
        n, width = queries.shape
        heads = log_decay.shape[0]
        hd = width // heads
        assert heads == 4
        flows = FX + steps
        hbm = pl.BlockSpec(memory_space=pltpu.HBM)
        state = (hd, hd)
        tile = (8, hd)
        out = jax.ShapeDtypeStruct((n, width), BF16)
        vm = pltpu.VMEM
        return pl.pallas_call(
            functools.partial(kernel, sizes, line, steps),
            out_shape=(out, out, out),
            in_specs=[hbm] * 4 + [pl.BlockSpec(memory_space=pltpu.VMEM), hbm],
            out_specs=(pl.BlockSpec(memory_space=pltpu.VMEM),) * 3,
            scratch_shapes=[
                vm((n, width), BF16), vm((n, width), BF16), vm((n, width), BF16), vm((n, width), BF16),
                vm((heads,) + state, BF16),
                vm((n, width), F32), vm((n, width), F32),
                vm((heads, 8, n), F32), vm((heads, n, 128), F32), vm((heads, 8, 128), F32), vm((heads,) + tile, F32),
                vm((heads,) + state, BF16),
                vm((flows,) + state, F32), vm((DX + steps,) + tile, F32),
                vm((2,) + state, F32), vm((2,) + tile, F32),
                vm((2,) + state, F32), vm((2,) + state, F32), vm((2,) + state, F32),
                vm((2,) + tile, F32), vm((2,) + tile, F32),
                vm((2,) + state, F32), vm((PIECES,) + tile, F32),
                vm((steps,) + state, F32), vm((steps,) + tile, F32), vm((steps + 1,) + tile, F32),
                vm(state, F32), vm((2,) + state, F32), vm((2,) + state, F32),
                pltpu.SemaphoreType.DMA((5,)),
                pltpu.SemaphoreType.DMA((flows, CHUNKS)), pltpu.SemaphoreType.DMA((flows, CHUNKS)),
                pltpu.SemaphoreType.DMA((DX + steps,)), pltpu.SemaphoreType.DMA((DX + steps,)),
            ],
            compiler_params=pltpu.CompilerParams(
                collective_id=0, has_side_effects=True, vmem_limit_bytes=50 * 1024 * 1024
            ),
        )(queries, keys, values, out_grad, log_decay, saved_states)

    seq = ("gx", "gy", "gz")
    return jax.shard_map(
        body,
        mesh=mesh,
        in_specs=(P(seq, None),) * 4 + (P(None, seq), P(seq, None, None, None)),
        out_specs=(P(seq, None),) * 3,
        check_vma=False,
    )
```

time: 47.4 us -> 44.7 us (0.943)
  Pallas kernels: 41.6 us -> 39.2 us
    pallas_call x1, Pallas kernels: 41.6 us -> 39.2 us  [body(): pl.pallas_call(functools.partial(kernel, sizes, line, steps), out_shape=(...]
where the time goes in v2:
time: 44.7 us; the launch traced here: 44.5 us
  Pallas kernels  39.2 us (88%)
  local copies, waits for them, and re-layouts  4.64 us (10%)
  between operations  0.65 us (1%)
    pallas_call x1, Pallas kernels, body(): pl.pallas_call(functools.partial(kernel, sizes, line, steps), out_shape=(...  39.2 us
    unnamed x7, local copies, waits for them, and re-layouts  4.64 us

profile of v2, /device:TPU:0, one launch (start us, length us, event | category | flops | bytes accessed | tf_op | source)
XLA Modules:
  0.0 44.5 jit_solution(14551373847544263314)
XLA Ops:
  0.6 0.0 copy-start
  0.6 1.0 %copy-done = bf16[1,4,256,256]{3,2,1,0:T(8,128)(2,1)S(1)} copy-done((bf16[1,4,256,256]{3,2,1,0:T(8,128)(2,1)S(1)}, bf16[1,4,256,256]{3,2,1,0:T(8,128)(2,1)}, u32[]{:S(2)}) %copy-start) | copy-done | bytes 524312
  1.7 0.0 copy-start.1
  1.7 0.7 %copy-done.1 = f32[4,512]{1,0:T(4,128)S(1)} copy-done((f32[4,512]{1,0:T(4,128)S(1)}, f32[4,512]{1,0:T(4,128)}, u32[]{:S(2)}) %copy-start.1) | copy-done | bytes 8216
  2.4 39.2 %shard_map.85 = (bf16[512,1024]{1,0:T(8,128)(2,1)S(1)}, bf16[512,1024]{1,0:T(8,128)(2,1)S(1)}, bf16[512,1024]{1,0:T(8,128)(2,1)S(1)}) custom-call(bf16[512,1024]{1,0:T(8,128)(2,1)} %q_hbm.1, bf16[512,1024]{1,0:T(8,128)(2,1)} %k_hbm.1, bf16[512,1024]{1,0:T(8,128)(2,1)} %v_hbm.1, bf16[512,1024]{1,0:T(8,128)(2,1)} %g_hbm.1, f32[4,512]{1,0:T(4,128)S(1)} %copy-done.1, ...), custom_call_target="tpu_custom_call" | custom-call | tf_op jit(solution)/shard_map/pallas_call | solution.py:499
  41.5 1.0 %copy.12 = bf16[512,1024]{1,0:T(8,128)(2,1)} copy(bf16[512,1024]{1,0:T(8,128)(2,1)S(1)} %get-tuple-element.6) | data formatting | bytes 2097152
  42.5 1.0 %copy.13 = bf16[512,1024]{1,0:T(8,128)(2,1)} copy(bf16[512,1024]{1,0:T(8,128)(2,1)S(1)} %get-tuple-element.7) | data formatting | bytes 2097152
  43.5 1.0 %copy.14 = bf16[512,1024]{1,0:T(8,128)(2,1)} copy(bf16[512,1024]{1,0:T(8,128)(2,1)S(1)} %get-tuple-element.8) | data formatting | bytes 2097152
Async XLA Ops:
  0.6 1.0 %copy-start = (bf16[1,4,256,256]{3,2,1,0:T(8,128)(2,1)S(1)}, bf16[1,4,256,256]{3,2,1,0:T(8,128)(2,1)}, u32[]{:S(2)}) copy-start(bf16[1,4,256,256]{3,2,1,0:T(8,128)(2,1)} %st_hbm.1) | copy-start | bytes 1572868
  1.7 0.7 %copy-start.1 = (f32[4,512]{1,0:T(4,128)S(1)}, f32[4,512]{1,0:T(4,128)}, u32[]{:S(2)}) copy-start(f32[4,512]{1,0:T(4,128)} %ld_ref.1) | copy-start | bytes 24580

commit v3 on v2

--- a/solution.py
+++ b/solution.py
@@ -12,7 +12,7 @@
 BF16 = jnp.bfloat16
 PIECES = 4
 PER_PIECE = 4
-DELAY = 3
+DELAY = 4
 TILE = 256
 NT = (((1,), (1,)), ((), ()))
 TN = (((0,), (0,)), ((), ()))
@@ -415,9 +415,9 @@
 
         for r in range(tiles):
 
-            @pl.when((t < heads * tiles) & (t % tiles == r))
-            def _():
-                block(t // tiles, r)
+            @pl.when((t < 2 * heads * tiles) & (t % (2 * tiles) == 2 * r))
+            def _():
+                block(t // (2 * tiles), r)
 
         return carry
 

time: 44.7 us -> 43.8 us (0.980)
  Pallas kernels: 39.2 us -> 38.3 us
    pallas_call x1, Pallas kernels: 39.2 us -> 38.3 us  [body(): pl.pallas_call(functools.partial(kernel, sizes, line, steps), out_shape=(...]
where the time goes in v3:
time: 43.8 us; the launch traced here: 43.6 us
  Pallas kernels  38.3 us (87%)
  local copies, waits for them, and re-layouts  4.64 us (11%)
  between operations  0.65 us (1%)
    pallas_call x1, Pallas kernels, body(): pl.pallas_call(functools.partial(kernel, sizes, line, steps), out_shape=(...  38.3 us
    unnamed x7, local copies, waits for them, and re-layouts  4.64 us

profile of v3, /device:TPU:0, one launch (start us, length us, event | category | flops | bytes accessed | tf_op | source)
XLA Modules:
  0.0 43.6 jit_solution(14251397683747455292)
XLA Ops:
  0.6 0.0 copy-start
  0.6 1.0 %copy-done = bf16[1,4,256,256]{3,2,1,0:T(8,128)(2,1)S(1)} copy-done((bf16[1,4,256,256]{3,2,1,0:T(8,128)(2,1)S(1)}, bf16[1,4,256,256]{3,2,1,0:T(8,128)(2,1)}, u32[]{:S(2)}) %copy-start) | copy-done | bytes 524312
  1.7 0.0 copy-start.1
  1.7 0.7 %copy-done.1 = f32[4,512]{1,0:T(4,128)S(1)} copy-done((f32[4,512]{1,0:T(4,128)S(1)}, f32[4,512]{1,0:T(4,128)}, u32[]{:S(2)}) %copy-start.1) | copy-done | bytes 8216
  2.4 38.3 %shard_map.85 = (bf16[512,1024]{1,0:T(8,128)(2,1)S(1)}, bf16[512,1024]{1,0:T(8,128)(2,1)S(1)}, bf16[512,1024]{1,0:T(8,128)(2,1)S(1)}) custom-call(bf16[512,1024]{1,0:T(8,128)(2,1)} %q_hbm.1, bf16[512,1024]{1,0:T(8,128)(2,1)} %k_hbm.1, bf16[512,1024]{1,0:T(8,128)(2,1)} %v_hbm.1, bf16[512,1024]{1,0:T(8,128)(2,1)} %g_hbm.1, f32[4,512]{1,0:T(4,128)S(1)} %copy-done.1, ...), custom_call_target="tpu_custom_call" | custom-call | tf_op jit(solution)/shard_map/pallas_call | solution.py:499
  40.7 1.0 %copy.12 = bf16[512,1024]{1,0:T(8,128)(2,1)} copy(bf16[512,1024]{1,0:T(8,128)(2,1)S(1)} %get-tuple-element.6) | data formatting | bytes 2097152
  41.7 1.0 %copy.13 = bf16[512,1024]{1,0:T(8,128)(2,1)} copy(bf16[512,1024]{1,0:T(8,128)(2,1)S(1)} %get-tuple-element.7) | data formatting | bytes 2097152
  42.6 1.0 %copy.14 = bf16[512,1024]{1,0:T(8,128)(2,1)} copy(bf16[512,1024]{1,0:T(8,128)(2,1)S(1)} %get-tuple-element.8) | data formatting | bytes 2097152
Async XLA Ops:
  0.6 1.0 %copy-start = (bf16[1,4,256,256]{3,2,1,0:T(8,128)(2,1)S(1)}, bf16[1,4,256,256]{3,2,1,0:T(8,128)(2,1)}, u32[]{:S(2)}) copy-start(bf16[1,4,256,256]{3,2,1,0:T(8,128)(2,1)} %st_hbm.1) | copy-start | bytes 1572868
  1.7 0.7 %copy-start.1 = (f32[4,512]{1,0:T(4,128)S(1)}, f32[4,512]{1,0:T(4,128)}, u32[]{:S(2)}) copy-start(f32[4,512]{1,0:T(4,128)} %ld_ref.1) | copy-start | bytes 24580
